TPU v7x, 128 devices: a whole 4x4x4 slice. The times are simulated.
128 devices in a mesh: ep: 32 (over z, x, core), dp: 4 (over y).
Axes of the slice: x: 4, y: 4, z: 4, core: 2. Of those that a mesh axis runs over, the one named last changes fastest.
Arguments:
- grad_out: float32 [16384, 1536], P(('ep', 'dp')), may hold values from -6 to 6
- tokens: bfloat16 [16384, 1536], P(('ep', 'dp')), may hold values from -6 to 6
- probs: float32 [16384, 4], P(('ep', 'dp')), may hold values from 0.1 to 0.5
- expert_ids: int32 [16384, 4], P(('ep', 'dp')), may hold values from 0 to 31, all different within a row; in each aligned block of 128 rows (0 to 127, 128 to 255, ...) at most 20 rows name the same one
- priority: int32 [128, 128], P(('ep', 'dp')), may hold values from 0 to 127, each once within a row
- cap_counts: int32 [32], replicated, may hold values from 10 to 20, as said below
- gate_weight: bfloat16 [32, 1536, 1536], P('ep'), may hold values from -0.15625 to 0.15625
- up_weight: bfloat16 [32, 1536, 1536], P('ep'), may hold values from -0.15625 to 0.15625
- down_weight: bfloat16 [32, 1536, 1536], P('ep'), may hold values from -0.15625 to 0.15625
Outputs:
- input_grad: bfloat16 [16384, 1536], P(('ep', 'dp'))
- prob_grad: float32 [16384, 4], P(('ep', 'dp'))
- gate_grad: bfloat16 [32, 1536, 1536], P('ep', 'dp')
- up_grad: bfloat16 [32, 1536, 1536], P('ep', 'dp')
- down_grad: bfloat16 [32, 1536, 1536], P('ep', 'dp')
Inputs may be any that keep to these rules, and one draw needn't show every extreme that they name: `expert_ids`: each row names 4 different experts; among the rows of one device no expert is named by more than 20 rows, and in some device some expert is named by exactly 20 rows. `priority`: each row orders the 128 tokens of one device, each number once. `cap_counts`: some expert has exactly 20.
All inputs are finite; a program needn't handle non-finite values. Where the computation divides by a largest or mean magnitude, that divisor is 1e-20 or more.
Results may differ from a plain program's by a relative error of at most 0.017.
Values may be sent and summed in bfloat16 or wider, within the bound.
A program may use at most 128 MiB of HBM per device.

v0:
```python
import jax
import jax.numpy as jnp
from jax import lax
from jax.sharding import PartitionSpec as P

sharpness = 1.702


def contract_last(first_op, second_op):
    return lax.dot_general(
        first_op, second_op, (((1,), (1,)), ((), ())), preferred_element_type=jnp.float32
    )


def contract_first(first_op, second_op):
    return lax.dot_general(
        first_op, second_op, (((0,), (0,)), ((), ())), preferred_element_type=jnp.float32
    )


def route_table(expert_ids, priority, cap_counts, buckets, capacity):
    ranking = priority[0]
    earlier = (ranking[None, :] < ranking[:, None]).astype(jnp.float32)
    expert_range = lax.broadcasted_iota(jnp.int32, (1, 1, buckets), 2)
    matches = (expert_ids[:, :, None] == expert_range).astype(jnp.float32)
    routed = jnp.sum(matches, axis=1)
    before = jnp.dot(earlier, routed)
    slot_rank = jnp.sum(matches * before[:, None, :], axis=2)
    keep_limit = jnp.sum(matches * cap_counts.astype(jnp.float32)[None, None, :], axis=2)
    slot_range = lax.broadcasted_iota(jnp.float32, (1, 1, capacity), 2)
    slot_hit = (
        (slot_rank[:, :, None] == slot_range) & (slot_rank < keep_limit)[:, :, None]
    ).astype(jnp.float32)
    placement = matches[:, :, :, None] * slot_hit[:, :, None, :]
    return placement.reshape(expert_ids.shape[0], expert_ids.shape[1], buckets * capacity)


def deltas(slot_x, slot_g, w_gate, w_up, w_down):
    gate_pre = contract_last(slot_x, w_gate)
    up_pre = contract_last(slot_x, w_up)
    act_delta = contract_last(slot_g, w_down)
    squash = jax.nn.sigmoid(sharpness * gate_pre)
    gated = gate_pre * squash
    activated = (up_pre + 1.0) * gated
    up_delta = (act_delta * gated).astype(jnp.bfloat16)
    gate_delta = (
        act_delta * (up_pre + 1.0) * (squash + sharpness * gate_pre * squash * (1.0 - squash))
    ).astype(jnp.bfloat16)
    return (activated, act_delta, gate_delta, up_delta)


def on_device(
    grad_out, tokens, probs, expert_ids, priority, cap_counts, gate_weight, up_weight, down_weight
):
    ep_size = lax.axis_size("ep")
    dp_size = lax.axis_size("dp")
    tok_rows, model_width = tokens.shape
    route_count = expert_ids.shape[1]
    capacity = 5 * route_count * tok_rows // (4 * ep_size)
    slot_rows = ep_size * capacity
    placement = route_table(expert_ids, priority, cap_counts, ep_size, capacity)
    slot_table = jnp.sum(placement, axis=1)
    table_low = slot_table.astype(jnp.bfloat16)
    row_scale = jnp.maximum(jnp.max(jnp.abs(grad_out), axis=1), 1.0)
    quantized = (grad_out / row_scale[:, None]).astype(jnp.bfloat16)
    send_prob = jnp.sum(placement * probs[:, :, None], axis=(0, 1))
    send_scale = jnp.sum(slot_table * row_scale[:, None], axis=0)
    send_x = jnp.einsum("ts,td->sd", table_low, tokens, preferred_element_type=jnp.float32).astype(
        jnp.bfloat16
    )
    send_g = (
        jnp.einsum("ts,td->sd", table_low, quantized, preferred_element_type=jnp.float32)
        * (send_prob * send_scale)[:, None]
    ).astype(jnp.bfloat16)
    bucket_shape = (ep_size, capacity, model_width)

    def exchange(a):
        return lax.all_to_all(a, "ep", split_axis=0, concat_axis=0, tiled=True)

    slot_x = exchange(send_x.reshape(bucket_shape)).reshape(slot_rows, model_width)
    all_x = lax.all_gather(slot_x, "dp", axis=0, tiled=True)
    slot_g = exchange(send_g.reshape(bucket_shape)).reshape(slot_rows, model_width)
    all_g = lax.all_gather(slot_g, "dp", axis=0, tiled=True)
    w_gate = gate_weight[0]
    w_up = up_weight[0]
    w_down = down_weight[0]
    activated, act_delta, gate_delta, up_delta = deltas(slot_x, slot_g, w_gate, w_up, w_down)
    slot_in = (
        jnp.dot(gate_delta, w_gate, preferred_element_type=jnp.float32)
        + jnp.dot(up_delta, w_up, preferred_element_type=jnp.float32)
    ).astype(jnp.bfloat16)
    slot_out = jnp.sum(activated * act_delta, axis=1)
    back_in = exchange(slot_in.reshape(bucket_shape))
    back_prob = exchange(slot_out.reshape(ep_size, capacity).astype(jnp.bfloat16))
    prob_grad = jnp.einsum("tks,s->tk", placement, back_prob.reshape(slot_rows)) / probs
    input_grad = jnp.einsum(
        "ts,sd->td",
        table_low,
        back_in.reshape(slot_rows, model_width),
        preferred_element_type=jnp.float32,
    ).astype(jnp.bfloat16)
    share = w_gate.shape[0] // dp_size
    first = lax.axis_index("dp") * share

    def mine(w):
        return lax.dynamic_slice_in_dim(w, first, share, 0)

    act_mine, _, gd_mine, ud_mine = deltas(all_x, all_g, mine(w_gate), mine(w_up), mine(w_down))
    gate_share = contract_first(gd_mine, all_x).astype(jnp.bfloat16)
    up_share = contract_first(ud_mine, all_x).astype(jnp.bfloat16)
    down_share = contract_first(act_mine.astype(jnp.bfloat16), all_g).astype(jnp.bfloat16)
    return (input_grad, prob_grad, gate_share[None], up_share[None], down_share[None])


def solution(mesh):
    return jax.shard_map(
        on_device,
        mesh=mesh,
        in_specs=(
            P(("ep", "dp"), None),
            P(("ep", "dp"), None),
            P(("ep", "dp"), None),
            P(("ep", "dp"), None),
            P(("ep", "dp"), None),
            P(),
            P("ep", None, None),
            P("ep", None, None),
            P("ep", None, None),
        ),
        out_specs=(
            P(("ep", "dp"), None),
            P(("ep", "dp"), None),
            P("ep", "dp", None),
            P("ep", "dp", None),
            P("ep", "dp", None),
        ),
        check_vma=False,
    )
```

profile of v0, /device:TPU:1, one launch (start us, length us, event | category | flops | bytes accessed | tf_op | source)
XLA Modules:
  0.0 248.0 jit_solution(7221112332950681031)
XLA Ops:
  7.2 0.0 copy-start
  7.2 0.0 all-gather.5.cloned.1.call-start
  7.2 0.7 convert_element_type.78
  7.9 0.7 fusion.39
  8.6 0.8 select_reduce_fusion
  9.4 0.9 fusion.40
  10.3 0.7 select_reduce_fusion.1
  11.1 1.3 abs_reduce_fusion
  12.4 1.0 fusion.24
  13.3 0.2 multiply_reduce_fusion.2
  13.5 0.1 copy.29
  13.6 1.9 convolution_convert_fusion
  15.6 2.5 reshape.94
  18.0 40.7 %all_to_all.24 = bf16[32,20,1536]{2,1,0:T(8,128)(2,1)} all-to-all(bf16[32,20,1536]{2,1,0:T(8,128)(2,1)S(1)} %reshape.94), channel_id=1, replica_groups=mesh['ep'=32,'dp'=4] {'ep'}, dimensions={0} | all-to-all | bytes 3932160 | tf_op jit(solution)/shard_map/all_to_all | solution.py:78
  58.7 4.1 %reshape.95 = bf16[640,1536]{1,0:T(8,128)(2,1)} reshape(bf16[32,20,1536]{2,1,0:T(8,128)(2,1)} %all_to_all.24) | data formatting | bytes 3932160 | tf_op jit(solution)/shard_map/reshape | solution.py:80
  62.8 0.0 all-gather.5.cloned.1.call-update
  62.8 0.0 all-gather.3.cloned.1.call-start
  62.9 0.1 copy.30
  62.9 0.1 mul.136
  63.1 2.1 multiply_convert_fusion.5
  65.2 2.5 reshape.92
  67.6 35.0 %all_to_all.25 = bf16[32,20,1536]{2,1,0:T(8,128)(2,1)} all-to-all(bf16[32,20,1536]{2,1,0:T(8,128)(2,1)S(1)} %reshape.92), channel_id=1, replica_groups=mesh['ep'=32,'dp'=4] {'ep'}, dimensions={0} | all-to-all | bytes 3932160 | tf_op jit(solution)/shard_map/all_to_all | solution.py:78
  102.6 4.1 %reshape.93 = bf16[640,1536]{1,0:T(8,128)(2,1)} reshape(bf16[32,20,1536]{2,1,0:T(8,128)(2,1)} %all_to_all.25) | data formatting | bytes 3932160 | tf_op jit(solution)/shard_map/reshape | solution.py:82
  106.8 0.0 all-gather.3.cloned.1.call-update
  106.8 0.0 slice-start.2
  106.8 5.3 %fusion.6 = f32[640,1536]{1,0:T(8,128)S(1)} fusion(bf16[640,1536]{1,0:T(8,128)(2,1)S(1)} %copy-done.2, bf16[1,1536,1536]{2,1,0:T(8,128)(2,1)} %param.16), kind=kOutput, calls=%fused_computation.6 | convolution fusion | flops 3019898880 | bytes 10616832 | tf_op jit(solution)/shard_map/dot_general | solution.py:10
  112.1 0.0 slice-start.3
  112.1 6.6 %fusion.2 = f32[640,1536]{1,0:T(8,128)S(1)} fusion(bf16[640,1536]{1,0:T(8,128)(2,1)S(1)} %copy-done.2, bf16[1,1536,1536]{2,1,0:T(8,128)(2,1)} %param.15), kind=kOutput, calls=%fused_computation.2 | convolution fusion | flops 3019898880 | bytes 10616832 | tf_op jit(solution)/shard_map/dot_general | solution.py:10
  118.8 5.4 %multiply_reduce_fusion = (bf16[640]{0:T(1024)(128)(2,1)S(1)}, f32[640,1536]{1,0:T(8,128)}) fusion(f32[640,1536]{1,0:T(8,128)S(1)} %fusion.6, f32[640,1536]{1,0:T(8,128)S(1)} %fusion.2, bf16[640,1536]{1,0:T(8,128)(2,1)S(1)} %copy-done.3, bf16[1,1536,1536]{2,1,0:T(8,128)(2,1)S(1)} %bitcast.64), kind=kOutput, calls=%fused_computation.15 | convolution fusion | flops 3028745728 | bytes 18482432 | tf_op jit(solution)/shard_map/dot_general | solution.py:10
  124.2 0.7 convert_element_type.97
  124.9 3.8 %all-to-all-start.3 = ((bf16[32,1,20]{2,1,0:T(2,128)(2,1)}), bf16[32,1,20]{2,1,0:T(2,128)(2,1)S(1)}, u32[]{:S(2)}, u32[]{:S(2)}) async-start(bf16[32,1,20]{2,1,0:T(2,128)(2,1)} %convert_element_type.97), calls=%async_computation.3 | async-start | bytes 32768 | tf_op jit(solution)/shard_map/all_to_all | solution.py:78
  128.8 8.9 %fusion = f32[640,1536]{1,0:T(8,128)S(1)} fusion(bf16[1,1536,1536]{2,1,0:T(8,128)(2,1)} %param.15, f32[640,1536]{1,0:T(8,128)} %get-tuple-element.12, f32[640,1536]{1,0:T(8,128)} %copy-done.9, f32[640,1536]{1,0:T(8,128)} %copy-done.11), kind=kOutput, calls=%fused_computation | convolution fusion | flops 3031695360 | bytes 20447232 | tf_op jit(solution)/shard_map/dot_general | solution.py:89
  137.7 5.8 %add_convert_fusion = bf16[640,1536]{1,0:T(8,128)(2,1)S(1)} fusion(f32[640,1536]{1,0:T(8,128)S(1)} %fusion, bf16[1,1536,1536]{2,1,0:T(8,128)(2,1)} %param.16, f32[640,1536]{1,0:T(8,128)S(1)} %copy-done.13, f32[640,1536]{1,0:T(8,128)S(1)} %copy-done.10), kind=kOutput, calls=%fused_computation.16 | convolution fusion | flops 3028746240 | bytes 18481152 | tf_op jit(solution)/shard_map/dot_general | solution.py:90
  143.6 0.0 copy-start.5
  143.6 2.1 reshape.96
  145.7 7.3 %all-to-all-start.2 = ((bf16[32,20,1536]{2,1,0:T(8,128)(2,1)}), bf16[32,20,1536]{2,1,0:T(8,128)(2,1)S(1)}, u32[]{:S(2)}, u32[]{:S(2)}) async-start(bf16[32,20,1536]{2,1,0:T(8,128)(2,1)} %reshape.96), calls=%async_computation.2 | async-start | bytes 4718592 | tf_op jit(solution)/shard_map/all_to_all | solution.py:78
  153.0 0.1 copy.33
  153.1 0.2 fusion.17
  153.4 0.6 div.20
  154.0 30.6 %all-to-all-done.2 = bf16[32,20,1536]{2,1,0:T(8,128)(2,1)S(1)} async-done(((bf16[32,20,1536]{2,1,0:T(8,128)(2,1)}), bf16[32,20,1536]{2,1,0:T(8,128)(2,1)S(1)}, u32[]{:S(2)}, u32[]{:S(2)}) %all-to-all-start.2) | async-done | bytes 1966112 | tf_op jit(solution)/shard_map/all_to_all | solution.py:78
  184.5 1.5 fusion.19
  186.1 9.9 %fusion.25 = f32[2560,384]{1,0:T(8,128)} fusion(bf16[2560,1536]{1,0:T(8,128)(2,1)} %all-gather.5.cloned.1.call-done, bf16[1,1536,1536]{2,1,0:T(8,128)(2,1)} %param.15, s32[]{:T(128)S(6)} %select_n.2), kind=kOutput, calls=%fused_computation.41 | convolution fusion | flops 3019898880 | bytes 12976132 | tf_op jit(solution)/shard_map/dot_general | solution.py:10
  196.0 7.5 %convolution_add_fusion = f32[2560,384]{1,0:T(8,128)} fusion(bf16[2560,1536]{1,0:T(8,128)(2,1)S(1)} %copy-done.6, bf16[1,1536,1536]{2,1,0:T(8,128)(2,1)} %param.16, s32[]{:T(128)S(6)} %select_n.2), kind=kOutput, calls=%fused_computation.10 | convolution fusion | flops 3020881920 | bytes 12976132 | tf_op jit(solution)/shard_map/dot_general | solution.py:10
  203.4 16.9 %all-gather.3.cloned.1.call-done = bf16[2560,1536]{1,0:T(8,128)(2,1)} async-done(((bf16[640,1536]{1,0:T(8,128)(2,1)}), bf16[2560,1536]{1,0:T(8,128)(2,1)}) %all-gather.3.cloned.1.call-update) | async-done | bytes 7864336 | tf_op jit(solution)/shard_map/all_gather | solution.py:83
  220.3 7.4 %fusion.28 = f32[2560,384]{1,0:T(8,128)S(1)} fusion(bf16[2560,1536]{1,0:T(8,128)(2,1)} %all-gather.3.cloned.1.call-done, bf16[1,1536,1536]{2,1,0:T(8,128)(2,1)} %param.17, s32[]{:T(128)S(6)} %select_n.2), kind=kOutput, calls=%fused_computation.44 | convolution fusion | flops 3019898880 | bytes 12976132 | tf_op jit(solution)/shard_map/dot_general | solution.py:10
  227.7 4.4 %fusion.15 = bf16[1,384,1536]{2,1,0:T(8,128)(2,1)} fusion(bf16[2560,1536]{1,0:T(8,128)(2,1)S(1)} %copy-done.7, f32[2560,384]{1,0:T(8,128)S(1)} %fusion.28, f32[2560,384]{1,0:T(8,128)S(1)} %copy-done.8), kind=kOutput, calls=%fused_computation.28 | convolution fusion | flops 3027369984 | bytes 16908288 | tf_op jit(solution)/shard_map/dot_general | solution.py:16
  232.2 4.5 %fusion.14 = bf16[1,384,1536]{2,1,0:T(8,128)(2,1)} fusion(bf16[2560,1536]{1,0:T(8,128)(2,1)S(1)} %copy-done.7, f32[2560,384]{1,0:T(8,128)S(1)} %fusion.28, f32[2560,384]{1,0:T(8,128)S(1)} %copy-done.12, f32[2560,384]{1,0:T(8,128)S(1)} %copy-done.8), kind=kOutput, calls=%fused_computation.27 | convolution fusion | flops 3031302144 | bytes 20840448 | tf_op jit(solution)/shard_map/dot_general | solution.py:16
  236.7 4.4 %fusion.16 = bf16[1,384,1536]{2,1,0:T(8,128)(2,1)} fusion(bf16[2560,1536]{1,0:T(8,128)(2,1)S(1)} %bitcast.62, f32[2560,384]{1,0:T(8,128)S(1)} %copy-done.12, f32[2560,384]{1,0:T(8,128)S(1)} %copy-done.8), kind=kOutput, calls=%fused_computation.29 | convolution fusion | flops 3027369984 | bytes 16908288 | tf_op jit(solution)/shard_map/dot_general | solution.py:16
  (41 shorter events, 0.1 us)
Async XLA Ops:
  7.2 6.5 %copy-start = (bf16[128,1536]{1,0:T(8,128)(2,1)S(1)}, bf16[128,1536]{1,0:T(8,128)(2,1)}, u32[]{:S(2)}) copy-start(bf16[128,1536]{1,0:T(8,128)(2,1)} %param.10) | copy-start | bytes 1179652
  7.2 178.9 %all-gather.5.cloned.1.call-start = ((), (), s32[]{:S(2)}) async-start(), calls=%async_computation.5 | async-start | bytes 9830400 | tf_op jit(solution)/shard_map/all_gather | solution.py:81
  58.7 4.3 %copy-start.4 = (f32[128,1536]{1,0:T(8,128)S(1)}, f32[128,1536]{1,0:T(8,128)}, u32[]{:S(2)}) copy-start(f32[128,1536]{1,0:T(8,128)} %param.9) | copy-start | bytes 2359300
  62.8 157.5 %all-gather.3.cloned.1.call-start = ((), (), s32[]{:S(2)}) async-start(), calls=%async_computation.4 | async-start | bytes 9830400 | tf_op jit(solution)/shard_map/all_gather | solution.py:83
  102.6 4.2 %copy-start.2 = (bf16[640,1536]{1,0:T(8,128)(2,1)S(1)}, bf16[640,1536]{1,0:T(8,128)(2,1)}, u32[]{:S(2)}) copy-start(bf16[640,1536]{1,0:T(8,128)(2,1)} %reshape.95) | copy-start | bytes 5898244
  106.8 12.0 %slice-start.2 = ((s8[4718592]{0:T(1024)(128)(4,1)}), s8[4194304]{0:T(1024)(128)(4,1)S(1)}, s32[]{:S(2)}) async-start(s8[4718592]{0:T(1024)(128)(4,1)} %bitcast.63), calls=%async_computation.8 | async-start | bytes 8388608
  112.1 6.7 %copy-start.11 = (f32[640,1536]{1,0:T(8,128)}, f32[640,1536]{1,0:T(8,128)S(1)}, u32[]{:S(2)}) copy-start(f32[640,1536]{1,0:T(8,128)S(1)} %fusion.6) | copy-start | bytes 11796484
  112.1 6.7 %copy-start.3 = (bf16[640,1536]{1,0:T(8,128)(2,1)S(1)}, bf16[640,1536]{1,0:T(8,128)(2,1)}, u32[]{:S(2)}) copy-start(bf16[640,1536]{1,0:T(8,128)(2,1)} %reshape.93) | copy-start | bytes 5898244
  112.1 6.7 %slice-start.3 = ((s8[4718592]{0:T(1024)(128)(4,1)}), s8[524288]{0:T(1024)(128)(4,1)S(1)}, s32[]{:S(2)}) async-start(s8[4718592]{0:T(1024)(128)(4,1)} %bitcast.63), calls=%async_computation.9 | async-start | bytes 1048576
  118.8 5.4 %copy-start.9 = (f32[640,1536]{1,0:T(8,128)}, f32[640,1536]{1,0:T(8,128)S(1)}, u32[]{:S(2)}) copy-start(f32[640,1536]{1,0:T(8,128)S(1)} %fusion.2) | copy-start | bytes 11796484
  124.9 20.7 %all-to-all-start.3 = ((bf16[32,1,20]{2,1,0:T(2,128)(2,1)}), bf16[32,1,20]{2,1,0:T(2,128)(2,1)S(1)}, u32[]{:S(2)}, u32[]{:S(2)}) async-start(bf16[32,1,20]{2,1,0:T(2,128)(2,1)} %convert_element_type.97), calls=%async_computation.3 | async-start | bytes 32768 | tf_op jit(solution)/shard_map/all_to_all | solution.py:78
  128.8 9.0 %copy-start.10 = (f32[640,1536]{1,0:T(8,128)S(1)}, f32[640,1536]{1,0:T(8,128)}, u32[]{:S(2)}) copy-start(f32[640,1536]{1,0:T(8,128)} %copy-done.9) | copy-start | bytes 11796484
  128.8 9.0 %copy-start.13 = (f32[640,1536]{1,0:T(8,128)S(1)}, f32[640,1536]{1,0:T(8,128)}, u32[]{:S(2)}) copy-start(f32[640,1536]{1,0:T(8,128)} %get-tuple-element.12) | copy-start | bytes 11796484
  143.6 9.8 %copy-start.5 = (f32[128,4]{0,1:T(4,128)S(1)}, f32[128,4]{0,1:T(4,128)}, u32[]{:S(2)}) copy-start(f32[128,4]{0,1:T(4,128)} %param.11) | copy-start | bytes 6148
  145.7 38.9 %all-to-all-start.2 = ((bf16[32,20,1536]{2,1,0:T(8,128)(2,1)}), bf16[32,20,1536]{2,1,0:T(8,128)(2,1)S(1)}, u32[]{:S(2)}, u32[]{:S(2)}) async-start(bf16[32,20,1536]{2,1,0:T(8,128)(2,1)} %reshape.96), calls=%async_computation.2 | async-start | bytes 4718592 | tf_op jit(solution)/shard_map/all_to_all | solution.py:78
  186.1 9.9 %copy-start.6 = (bf16[2560,1536]{1,0:T(8,128)(2,1)S(1)}, bf16[2560,1536]{1,0:T(8,128)(2,1)}, u32[]{:S(2)}) copy-start(bf16[2560,1536]{1,0:T(8,128)(2,1)} %all-gather.5.cloned.1.call-done) | copy-start | bytes 23592964
  220.3 7.4 %copy-start.7 = (bf16[2560,1536]{1,0:T(8,128)(2,1)S(1)}, bf16[2560,1536]{1,0:T(8,128)(2,1)}, u32[]{:S(2)}) copy-start(bf16[2560,1536]{1,0:T(8,128)(2,1)} %all-gather.5.cloned.1.call-done) | copy-start | bytes 23592964
  220.3 7.4 %copy-start.8 = (f32[2560,384]{1,0:T(8,128)S(1)}, f32[2560,384]{1,0:T(8,128)}, u32[]{:S(2)}) copy-start(f32[2560,384]{1,0:T(8,128)} %fusion.25) | copy-start | bytes 11796484
  227.7 4.5 %copy-start.12 = (f32[2560,384]{1,0:T(8,128)S(1)}, f32[2560,384]{1,0:T(8,128)}, u32[]{:S(2)}) copy-start(f32[2560,384]{1,0:T(8,128)} %convolution_add_fusion) | copy-start | bytes 11796484
  227.7 9.0 %slice-start = ((s8[7864320]{0:T(1024)(128)(4,1)}), s8[4194304]{0:T(1024)(128)(4,1)S(1)}, s32[]{:S(2)}) async-start(s8[7864320]{0:T(1024)(128)(4,1)} %bitcast.61), calls=%async_computation.6 | async-start | bytes 8388608
  232.2 4.6 %slice-start.1 = ((s8[7864320]{0:T(1024)(128)(4,1)}), s8[3670016]{0:T(1024)(128)(4,1)S(1)}, s32[]{:S(2)}) async-start(s8[7864320]{0:T(1024)(128)(4,1)} %bitcast.61), calls=%async_computation.7 | async-start | bytes 7340032
  236.7 4.4 %copy-start.1 = (bf16[128,1536]{1,0:T(8,128)(2,1)S(1)}, bf16[128,1536]{1,0:T(8,128)(2,1)}, u32[]{:S(2)}) copy-start(bf16[128,1536]{1,0:T(8,128)(2,1)} %param.10) | copy-start | bytes 1179652
Sparse Core Ops, SparseCore 0:
  62.9 76.0 all-gather.4
  140.7 79.5 all-gather.2
where the time goes:
time: 249 us; the launch traced here: 248 us
  matrix products  76.9 us (31%)
  blocking collectives  75.7 us (30%)
  waiting for transfers between devices  47.5 us (19%)
  local copies, waits for them, and re-layouts  16.4 us (7%)
  between operations  14.4 us (6%)
  starting transfers between devices  11.2 us (4%)
  other arithmetic  5.9 us (2%)
    all_to_all x2, blocking collectives, exchange(): return lax.all_to_all(a, 'ep', split_axis=0, concat_axis=0, tiled=True)  75.7 us
    dot_general x6, matrix products, contract_last(): lax.dot_general(first_op, second_op, (((1,), (1,)), ((), ())), preferred_...  42 us
    all_to_all x2, waiting for transfers between devices, exchange(): return lax.all_to_all(a, 'ep', split_axis=0, concat_axis=0, tiled=True)  30.6 us
    all_gather x1, waiting for transfers between devices, on_device(): all_g = lax.all_gather(slot_g, 'dp', axis=0, tiled=True)  16.9 us
    dot_general x3, matrix products, contract_first(): lax.dot_general(first_op, second_op, (((0,), (0,)), ((), ())), preferred_...  13.4 us
    all_to_all x2, starting transfers between devices, exchange(): return lax.all_to_all(a, 'ep', split_axis=0, concat_axis=0, tiled=True)  11.1 us
    dot_general x1, matrix products, on_device(): jnp.dot(gate_delta, w_gate, preferred_element_type=jnp.float32)  8.95 us
    dot_general x1, matrix products, on_device(): jnp.dot(up_delta, w_up, preferred_element_type=jnp.float32)  5.8 us
  transfers between devices with their start and end apart: 4, of which 2 were waited for; matrix products, arithmetic and copies ran while one was open for 26% of the time, Pallas kernels for 0%

commit v1 on v0

--- a/solution.py
+++ b/solution.py
@@ -78,9 +78,12 @@
         return lax.all_to_all(a, "ep", split_axis=0, concat_axis=0, tiled=True)
 
     slot_x = exchange(send_x.reshape(bucket_shape)).reshape(slot_rows, model_width)
-    all_x = lax.all_gather(slot_x, "dp", axis=0, tiled=True)
     slot_g = exchange(send_g.reshape(bucket_shape)).reshape(slot_rows, model_width)
-    all_g = lax.all_gather(slot_g, "dp", axis=0, tiled=True)
+    all_x, all_g = jnp.split(
+        lax.all_gather(jnp.concatenate([slot_x, slot_g], axis=1), "dp", axis=0, tiled=True),
+        [slot_x.shape[1]],
+        axis=1,
+    )
     w_gate = gate_weight[0]
     w_up = up_weight[0]
     w_down = down_weight[0]

time: 249 us -> 294 us (1.18)
  waiting for transfers between devices: 47.5 us -> 146 us
  blocking collectives: 75.7 us -> 0 us
  starting transfers between devices: 11.2 us -> 29 us
  other arithmetic: 5.9 us -> 9.78 us
    all_to_all x2 -> x0, blocking collectives: 75.7 us -> none  [exchange(): return lax.all_to_all(a, 'ep', split_axis=0, concat_axis=0, tiled=True)]
    all_to_all x2 -> x4, waiting for transfers between devices: 30.6 us -> 83.9 us  [exchange(): return lax.all_to_all(a, 'ep', split_axis=0, concat_axis=0, tiled=True)]
    all_gather x2 -> x1, waiting for transfers between devices: 16.9 us -> 62.2 us  [on_device(): lax.all_gather(jnp.concatenate([slot_x, slot_g], axis=1), 'dp', axis=0, t...]
    all_to_all x2 -> x4, starting transfers between devices: 11.1 us -> 29 us  [exchange(): return lax.all_to_all(a, 'ep', split_axis=0, concat_axis=0, tiled=True)]
    dot_general x3, matrix products: 13.4 us -> 18.8 us  [contract_first(): lax.dot_general(first_op, second_op, (((0,), (0,)), ((), ())), preferred_...]
    dot_general x6, matrix products: 42 us -> 38 us  [contract_last(): lax.dot_general(first_op, second_op, (((1,), (1,)), ((), ())), preferred_...]
    concatenate x0 -> x1, other arithmetic: none -> 3.87 us  [on_device(): jnp.concatenate([slot_x, slot_g], axis=1)]
  transfers between devices with their start and end apart: 4 -> 5, of which waited for: 2 -> 4; matrix products, arithmetic and copies ran while one was open for 26% -> 16% of each run, Pallas kernels for 0% -> 0%
where the time goes in v1:
time: 294 us
  waiting for transfers between devices  146 us (50%)
  matrix products  78.2 us (27%)
  starting transfers between devices  29 us (10%)
  local copies, waits for them, and re-layouts  16.1 us (5%)
  between operations  14.3 us (5%)
  other arithmetic  9.78 us (3%)
    all_to_all x4, waiting for transfers between devices, exchange(): return lax.all_to_all(a, 'ep', split_axis=0, concat_axis=0, tiled=True)  83.9 us
    all_gather x1, waiting for transfers between devices, on_device(): lax.all_gather(jnp.concatenate([slot_x, slot_g], axis=1), 'dp', axis=0, t...  62.2 us
    dot_general x6, matrix products, contract_last(): lax.dot_general(first_op, second_op, (((1,), (1,)), ((), ())), preferred_...  38 us
    all_to_all x4, starting transfers between devices, exchange(): return lax.all_to_all(a, 'ep', split_axis=0, concat_axis=0, tiled=True)  29 us
    dot_general x3, matrix products, contract_first(): lax.dot_general(first_op, second_op, (((0,), (0,)), ((), ())), preferred_...  18.8 us
    dot_general x1, matrix products, on_device(): jnp.dot(gate_delta, w_gate, preferred_element_type=jnp.float32)  8.99 us
  transfers between devices with their start and end apart: 5, of which 4 were waited for; matrix products, arithmetic and copies ran while one was open for 16% of the time, Pallas kernels for 0%

profile of v1, /device:TPU:1, one launch (start us, length us, event | category | flops | bytes accessed | tf_op | source)
XLA Modules:
  0.0 293.5 jit_solution(14144640980499221936)
XLA Ops:
  7.2 0.0 copy-start
  7.2 0.7 convert_element_type.78
  7.9 0.7 fusion.68
  8.6 0.8 select_reduce_fusion
  9.4 0.9 fusion.69
  10.3 0.7 select_reduce_fusion.1
  11.0 1.3 abs_reduce_fusion
  12.3 1.0 fusion.55
  13.3 0.2 multiply_reduce_fusion.2
  13.5 0.1 copy.29
  13.6 0.7 convolution_convert_fusion
  14.2 2.1 reshape.94
  16.3 9.4 %all-to-all-start.1 = ((bf16[32,20,1536]{2,1,0:T(8,128)(2,1)}), bf16[32,20,1536]{2,1,0:T(8,128)(2,1)S(1)}, u32[]{:S(2)}, u32[]{:S(2)}) async-start(bf16[32,20,1536]{2,1,0:T(8,128)(2,1)} %reshape.94), calls=%async_computation.1 | async-start | bytes 4718592 | tf_op jit(solution)/shard_map/all_to_all | solution.py:78
  25.8 0.1 copy.30
  25.9 0.1 mul.136
  26.0 3.2 %multiply_convert_fusion.5 = bf16[640,1536]{1,0:T(8,128)(2,1)} fusion(bf16[128,640]{0,1:T(8,128)(2,1)S(1)} %convert_element_type.81, f32[640]{0:T(1024)S(1)} %mul.136, f32[128,1536]{1,0:T(8,128)} %param.9, f32[128]{0:T(128)S(1)} %broadcast_maximum_fusion), kind=kOutput, calls=%fused_computation.33 | convolution fusion | flops 254017536 | bytes 2919424 | tf_op jit(solution)/shard_map/ts,td->sd/dot_general | solution.py:72
  29.2 4.0 %reshape.92 = bf16[32,20,1536]{2,1,0:T(8,128)(2,1)} reshape(bf16[640,1536]{1,0:T(8,128)(2,1)} %multiply_convert_fusion.5) | data formatting | bytes 3932160 | tf_op jit(solution)/shard_map/reshape | solution.py:81
  33.1 24.1 %all-to-all-done.1 = bf16[32,20,1536]{2,1,0:T(8,128)(2,1)S(1)} async-done(((bf16[32,20,1536]{2,1,0:T(8,128)(2,1)}), bf16[32,20,1536]{2,1,0:T(8,128)(2,1)S(1)}, u32[]{:S(2)}, u32[]{:S(2)}) %all-to-all-start.1) | async-done | bytes 1966112 | tf_op jit(solution)/shard_map/all_to_all | solution.py:78
  57.3 6.3 %all-to-all-start = ((bf16[32,20,1536]{2,1,0:T(8,128)(2,1)}), bf16[32,20,1536]{2,1,0:T(8,128)(2,1)}, u32[]{:S(2)}, u32[]{:S(2)}) async-start(bf16[32,20,1536]{2,1,0:T(8,128)(2,1)} %reshape.92), calls=%async_computation | async-start | bytes 4718592 | tf_op jit(solution)/shard_map/all_to_all | solution.py:78
  63.5 0.0 all-gather.2.cloned.1.call-start
  63.6 2.0 reshape.95
  65.6 29.2 %all-to-all-done = bf16[32,20,1536]{2,1,0:T(8,128)(2,1)} async-done(((bf16[32,20,1536]{2,1,0:T(8,128)(2,1)}), bf16[32,20,1536]{2,1,0:T(8,128)(2,1)}, u32[]{:S(2)}, u32[]{:S(2)}) %all-to-all-start) | async-done | bytes 1966112 | tf_op jit(solution)/shard_map/all_to_all | solution.py:78
  94.8 4.0 %reshape.93 = bf16[640,1536]{1,0:T(8,128)(2,1)} reshape(bf16[32,20,1536]{2,1,0:T(8,128)(2,1)} %all-to-all-done) | data formatting | bytes 3932160 | tf_op jit(solution)/shard_map/reshape | solution.py:81
  98.9 3.9 %pad_maximum_fusion = bf16[640,3072]{1,0:T(8,128)(2,1)} fusion(bf16[640,1536]{1,0:T(8,128)(2,1)} %reshape.93, bf16[640,1536]{1,0:T(8,128)(2,1)S(1)} %copy-done.2), kind=kLoop, calls=%fused_computation.23 | loop fusion | flops 7864320 | bytes 7864320 | tf_op jit(solution)/shard_map/concatenate | solution.py:83
  102.7 0.0 all-gather.2.cloned.1.call-update
  102.8 5.3 %fusion.18 = f32[640,1536]{1,0:T(8,128)S(1)} fusion(bf16[640,1536]{1,0:T(8,128)(2,1)S(1)} %copy-done.2, bf16[1,1536,1536]{2,1,0:T(8,128)(2,1)} %param.16), kind=kOutput, calls=%fused_computation.18 | convolution fusion | flops 3019898880 | bytes 10616832 | tf_op jit(solution)/shard_map/dot_general | solution.py:10
  108.1 0.0 slice-start.1
  108.1 6.7 %fusion.14 = f32[640,1536]{1,0:T(8,128)S(1)} fusion(bf16[640,1536]{1,0:T(8,128)(2,1)S(1)} %copy-done.2, bf16[1,1536,1536]{2,1,0:T(8,128)(2,1)} %param.15), kind=kOutput, calls=%fused_computation.14 | convolution fusion | flops 3019898880 | bytes 10616832 | tf_op jit(solution)/shard_map/dot_general | solution.py:10
  114.9 5.5 %multiply_reduce_fusion = (bf16[640]{0:T(1024)(128)(2,1)S(1)}, f32[640,1536]{1,0:T(8,128)}) fusion(f32[640,1536]{1,0:T(8,128)S(1)} %fusion.18, f32[640,1536]{1,0:T(8,128)S(1)} %fusion.14, bf16[640,1536]{1,0:T(8,128)(2,1)S(1)} %copy-done.3, bf16[1,1536,1536]{2,1,0:T(8,128)(2,1)S(1)} %bitcast.56), kind=kOutput, calls=%fused_computation.28 | convolution fusion | flops 3028745728 | bytes 18482432 | tf_op jit(solution)/shard_map/dot_general | solution.py:10
  120.4 0.7 convert_element_type.97
  121.1 5.8 %all-to-all-start.3 = ((bf16[32,1,20]{2,1,0:T(2,128)(2,1)}), bf16[32,1,20]{2,1,0:T(2,128)(2,1)S(1)}, u32[]{:S(2)}, u32[]{:S(2)}) async-start(bf16[32,1,20]{2,1,0:T(2,128)(2,1)} %convert_element_type.97), calls=%async_computation.3 | async-start | bytes 32768 | tf_op jit(solution)/shard_map/all_to_all | solution.py:78
  126.9 9.0 %fusion.12 = f32[640,1536]{1,0:T(8,128)S(1)} fusion(bf16[1,1536,1536]{2,1,0:T(8,128)(2,1)} %param.15, f32[640,1536]{1,0:T(8,128)} %get-tuple-element.12, f32[640,1536]{1,0:T(8,128)} %copy-done.6, f32[640,1536]{1,0:T(8,128)} %copy-done.8), kind=kOutput, calls=%fused_computation.12 | convolution fusion | flops 3031695360 | bytes 20447232 | tf_op jit(solution)/shard_map/dot_general | solution.py:92
  135.9 5.8 %add_convert_fusion = bf16[640,1536]{1,0:T(8,128)(2,1)S(1)} fusion(f32[640,1536]{1,0:T(8,128)S(1)} %fusion.12, bf16[1,1536,1536]{2,1,0:T(8,128)(2,1)} %param.16, f32[640,1536]{1,0:T(8,128)S(1)} %copy-done.9, f32[640,1536]{1,0:T(8,128)S(1)} %copy-done.7), kind=kOutput, calls=%fused_computation.29 | convolution fusion | flops 3028746240 | bytes 18481152 | tf_op jit(solution)/shard_map/dot_general | solution.py:93
  141.7 2.1 reshape.96
  143.8 7.5 %all-to-all-start.2 = ((bf16[32,20,1536]{2,1,0:T(8,128)(2,1)}), bf16[32,20,1536]{2,1,0:T(8,128)(2,1)S(1)}, u32[]{:S(2)}, u32[]{:S(2)}) async-start(bf16[32,20,1536]{2,1,0:T(8,128)(2,1)} %reshape.96), calls=%async_computation.2 | async-start | bytes 4718592 | tf_op jit(solution)/shard_map/all_to_all | solution.py:78
  151.3 0.1 copy.33
  151.4 0.2 fusion.47
  151.6 0.6 div.20
  152.2 30.6 %all-to-all-done.2 = bf16[32,20,1536]{2,1,0:T(8,128)(2,1)S(1)} async-done(((bf16[32,20,1536]{2,1,0:T(8,128)(2,1)}), bf16[32,20,1536]{2,1,0:T(8,128)(2,1)S(1)}, u32[]{:S(2)}, u32[]{:S(2)}) %all-to-all-start.2) | async-done | bytes 1966112 | tf_op jit(solution)/shard_map/all_to_all | solution.py:78
  182.8 1.5 fusion.49
  184.4 62.2 %all-gather.2.cloned.1.call-done = bf16[2560,3072]{1,0:T(8,128)(2,1)} async-done(((bf16[640,3072]{1,0:T(8,128)(2,1)}), bf16[2560,3072]{1,0:T(8,128)(2,1)}) %all-gather.2.cloned.1.call-update) | async-done | bytes 15728656 | tf_op jit(solution)/shard_map/all_gather | solution.py:83
  246.5 7.4 %fusion.2 = f32[2560,384]{1,0:T(8,128)S(1)} fusion(bf16[2560,3072]{1,0:T(8,128)(2,1)} %all-gather.2.cloned.1.call-done, bf16[1,1536,1536]{2,1,0:T(8,128)(2,1)} %param.17, s32[]{:T(128)S(6)} %select_n.2), kind=kOutput, calls=%fused_computation.2 | convolution fusion | flops 3019898880 | bytes 12976132 | tf_op jit(solution)/shard_map/dot_general | solution.py:10
  253.9 0.7 copy-done.5
  254.7 7.6 %fusion.22 = f32[2560,384]{1,0:T(8,128)} fusion(bf16[2560,3072]{1,0:T(8,128)(2,1)S(1)} %copy-done.5, bf16[1,1536,1536]{2,1,0:T(8,128)(2,1)} %param.16, s32[]{:T(128)S(6)} %select_n.2), kind=kOutput, calls=%fused_computation.22 | convolution fusion | flops 3020881920 | bytes 12976132 | tf_op jit(solution)/shard_map/dot_general | solution.py:10
  262.3 5.6 %fusion.8 = f32[2560,384]{1,0:T(8,128)S(1)} fusion(bf16[2560,3072]{1,0:T(8,128)(2,1)S(1)} %copy-done.5, bf16[1,1536,1536]{2,1,0:T(8,128)(2,1)} %param.15, s32[]{:T(128)S(6)} %select_n.2), kind=kOutput, calls=%fused_computation.8 | convolution fusion | flops 3019898880 | bytes 12976132 | tf_op jit(solution)/shard_map/dot_general | solution.py:10
  267.8 4.6 %fusion.41 = bf16[1,384,1536]{2,1,0:T(8,128)(2,1)} fusion(bf16[2560,3072]{1,0:T(8,128)(2,1)S(1)} %copy-done.5, f32[2560,384]{1,0:T(8,128)S(1)} %fusion.2, f32[2560,384]{1,0:T(8,128)S(1)} %fusion.8), kind=kOutput, calls=%fused_computation.41 | convolution fusion | flops 3027369984 | bytes 16908288 | tf_op jit(solution)/shard_map/dot_general | solution.py:16
  272.5 7.4 %fusion.44 = bf16[1,384,1536]{2,1,0:T(8,128)(2,1)} fusion(bf16[2560,3072]{1,0:T(8,128)(2,1)S(1)} %copy-done.5, f32[2560,384]{1,0:T(8,128)S(1)} %fusion.2, f32[2560,384]{1,0:T(8,128)} %fusion.22, f32[2560,384]{1,0:T(8,128)S(1)} %fusion.8), kind=kOutput, calls=%fused_computation.42 | convolution fusion | flops 3031302144 | bytes 20840448 | tf_op jit(solution)/shard_map/dot_general | solution.py:16
  279.9 6.8 %fusion.38 = bf16[1,384,1536]{2,1,0:T(8,128)(2,1)} fusion(bf16[2560,3072]{1,0:T(8,128)(2,1)S(1)} %copy-done.5, f32[2560,384]{1,0:T(8,128)} %fusion.22, f32[2560,384]{1,0:T(8,128)S(1)} %fusion.8), kind=kOutput, calls=%fused_computation.40 | convolution fusion | flops 3027369984 | bytes 16908288 | tf_op jit(solution)/shard_map/dot_general | solution.py:16
  (28 shorter events, 0.1 us)
Async XLA Ops:
  7.2 6.4 %copy-start = (bf16[128,1536]{1,0:T(8,128)(2,1)S(1)}, bf16[128,1536]{1,0:T(8,128)(2,1)}, u32[]{:S(2)}) copy-start(bf16[128,1536]{1,0:T(8,128)(2,1)} %param.10) | copy-start | bytes 1179652
  16.3 40.9 %all-to-all-start.1 = ((bf16[32,20,1536]{2,1,0:T(8,128)(2,1)}), bf16[32,20,1536]{2,1,0:T(8,128)(2,1)S(1)}, u32[]{:S(2)}, u32[]{:S(2)}) async-start(bf16[32,20,1536]{2,1,0:T(8,128)(2,1)} %reshape.94), calls=%async_computation.1 | async-start | bytes 4718592 | tf_op jit(solution)/shard_map/all_to_all | solution.py:78
  57.3 37.6 %all-to-all-start = ((bf16[32,20,1536]{2,1,0:T(8,128)(2,1)}), bf16[32,20,1536]{2,1,0:T(8,128)(2,1)}, u32[]{:S(2)}, u32[]{:S(2)}) async-start(bf16[32,20,1536]{2,1,0:T(8,128)(2,1)} %reshape.92), calls=%async_computation | async-start | bytes 4718592 | tf_op jit(solution)/shard_map/all_to_all | solution.py:78
  63.5 183.0 %all-gather.2.cloned.1.call-start = ((), (), s32[]{:S(2)}) async-start(), calls=%async_computation.4 | async-start | bytes 19660800 | tf_op jit(solution)/shard_map/all_gather | solution.py:83
  65.6 33.2 %copy-start.2 = (bf16[640,1536]{1,0:T(8,128)(2,1)S(1)}, bf16[640,1536]{1,0:T(8,128)(2,1)}, u32[]{:S(2)}) copy-start(bf16[640,1536]{1,0:T(8,128)(2,1)} %reshape.95) | copy-start | bytes 5898244
  102.8 12.1 %slice-start = ((s8[4718592]{0:T(1024)(128)(4,1)}), s8[4194304]{0:T(1024)(128)(4,1)S(1)}, s32[]{:S(2)}) async-start(s8[4718592]{0:T(1024)(128)(4,1)} %bitcast.55), calls=%async_computation.5 | async-start | bytes 8388608
  108.1 6.8 %copy-start.8 = (f32[640,1536]{1,0:T(8,128)}, f32[640,1536]{1,0:T(8,128)S(1)}, u32[]{:S(2)}) copy-start(f32[640,1536]{1,0:T(8,128)S(1)} %fusion.18) | copy-start | bytes 11796484
  108.1 6.8 %copy-start.3 = (bf16[640,1536]{1,0:T(8,128)(2,1)S(1)}, bf16[640,1536]{1,0:T(8,128)(2,1)}, u32[]{:S(2)}) copy-start(bf16[640,1536]{1,0:T(8,128)(2,1)} %reshape.93) | copy-start | bytes 5898244
  108.1 6.8 %slice-start.1 = ((s8[4718592]{0:T(1024)(128)(4,1)}), s8[524288]{0:T(1024)(128)(4,1)S(1)}, s32[]{:S(2)}) async-start(s8[4718592]{0:T(1024)(128)(4,1)} %bitcast.55), calls=%async_computation.6 | async-start | bytes 1048576
  114.9 5.5 %copy-start.6 = (f32[640,1536]{1,0:T(8,128)}, f32[640,1536]{1,0:T(8,128)S(1)}, u32[]{:S(2)}) copy-start(f32[640,1536]{1,0:T(8,128)S(1)} %fusion.14) | copy-start | bytes 11796484
  121.1 22.7 %all-to-all-start.3 = ((bf16[32,1,20]{2,1,0:T(2,128)(2,1)}), bf16[32,1,20]{2,1,0:T(2,128)(2,1)S(1)}, u32[]{:S(2)}, u32[]{:S(2)}) async-start(bf16[32,1,20]{2,1,0:T(2,128)(2,1)} %convert_element_type.97), calls=%async_computation.3 | async-start | bytes 32768 | tf_op jit(solution)/shard_map/all_to_all | solution.py:78
  126.9 9.0 %copy-start.7 = (f32[640,1536]{1,0:T(8,128)S(1)}, f32[640,1536]{1,0:T(8,128)}, u32[]{:S(2)}) copy-start(f32[640,1536]{1,0:T(8,128)} %copy-done.6) | copy-start | bytes 11796484
  126.9 9.0 %copy-start.9 = (f32[640,1536]{1,0:T(8,128)S(1)}, f32[640,1536]{1,0:T(8,128)}, u32[]{:S(2)}) copy-start(f32[640,1536]{1,0:T(8,128)} %get-tuple-element.12) | copy-start | bytes 11796484
  141.7 9.9 %copy-start.4 = (f32[128,4]{0,1:T(4,128)S(1)}, f32[128,4]{0,1:T(4,128)}, u32[]{:S(2)}) copy-start(f32[128,4]{0,1:T(4,128)} %param.11) | copy-start | bytes 6148
  143.8 39.0 %all-to-all-start.2 = ((bf16[32,20,1536]{2,1,0:T(8,128)(2,1)}), bf16[32,20,1536]{2,1,0:T(8,128)(2,1)S(1)}, u32[]{:S(2)}, u32[]{:S(2)}) async-start(bf16[32,20,1536]{2,1,0:T(8,128)(2,1)} %reshape.96), calls=%async_computation.2 | async-start | bytes 4718592 | tf_op jit(solution)/shard_map/all_to_all | solution.py:78
  246.5 8.1 %copy-start.5 = (bf16[2560,3072]{1,0:T(8,128)(2,1)S(1)}, bf16[2560,3072]{1,0:T(8,128)(2,1)}, u32[]{:S(2)}) copy-start(bf16[2560,3072]{1,0:T(8,128)(2,1)} %all-gather.2.cloned.1.call-done) | copy-start | bytes 47185924
  279.9 6.8 %copy-start.1 = (bf16[128,1536]{1,0:T(8,128)(2,1)S(1)}, bf16[128,1536]{1,0:T(8,128)(2,1)}, u32[]{:S(2)}) copy-start(bf16[128,1536]{1,0:T(8,128)(2,1)} %param.10) | copy-start | bytes 1179652
Sparse Core Ops, SparseCore 0:
  102.9 143.5 all-gather.1
